TPU v7x, 32 devices: a whole 2x2x4 slice. The times are simulated.
32 devices in a mesh: zero: 8 (over z, x), model: 4 (over y, core).
Axes of the slice: x: 2, y: 2, z: 4, core: 2. Of those that a mesh axis runs over, the one named last changes fastest.
Arguments:
- w_query: bfloat16 [4096, 4096], P('zero', 'model'), may hold values from -0.125 to 0.125
- low_query: bfloat16 [4096, 16], P('zero'), may hold values from -0.09375 to 0.09375
- high_query: bfloat16 [16, 4096], P(None, 'model'), may hold values from -1.5 to 1.5
- w_key: bfloat16 [4096, 4096], P('zero', 'model'), may hold values from -0.125 to 0.125
- low_key: bfloat16 [4096, 16], P('zero'), may hold values from -0.09375 to 0.09375
- high_key: bfloat16 [16, 4096], P(None, 'model'), may hold values from -1.5 to 1.5
- w_value: bfloat16 [4096, 4096], P('zero', 'model'), may hold values from -0.125 to 0.125
- low_value: bfloat16 [4096, 16], P('zero'), may hold values from -0.09375 to 0.09375
- high_value: bfloat16 [16, 4096], P(None, 'model'), may hold values from -1.5 to 1.5
- norm_train: float32 [4096], P(('zero', 'model')), may hold values from 0.25 to 1.75
- norm_step: float32 [4096], P(('zero', 'model')), may hold values from -0.3 to 0.3
Outputs:
- serving_query: bfloat16 [4096, 4096], P(None, 'model')
- serving_key: bfloat16 [4096, 4096], P(None, 'model')
- serving_value: bfloat16 [4096, 4096], P(None, 'model')
- factor_query: float32 [4096], P('model')
- factor_key: float32 [4096], P('model')
- factor_value: float32 [4096], P('model')
- serve_norm: bfloat16 [4096], replicated
All inputs are finite; a program needn't handle non-finite values. Where the computation divides by a largest or mean magnitude, that divisor is 1e-20 or more.
Results may differ from a plain program's by a relative error of at most 0.001.
Values may be sent and summed in bfloat16 or wider, within the bound.
A program may use at most 128 MiB of HBM per device.

v0:
```python
import functools

import jax
import jax.numpy as jnp
from jax import lax
from jax.experimental import pallas as pl
from jax.experimental.pallas import tpu as pltpu
from jax.sharding import PartitionSpec as P

MESH = pl.DeviceIdType.MESH
mix_rate = 0.5
VMEM_MOST = 67_043_328
SPARE = 65_536
COLUMNS = 2
PIECES = 6
WRITES = 4
FIRST = 2


def queues_of(z, length):
    every = [PIECES] + list(range(PIECES))
    late = list(range(PIECES // 2, PIECES))
    early = [c for c in every if c not in late]
    out = {"up": [], "down": [], "side": []}
    if z < length - 1:
        out["up"] += [(z - s, 0, c) for s in range(z + 1) for c in every]
        if z == 0:
            out["up"] += [(0, 1, c) for c in every]
        if z == length - 2:
            out["up"] += [(z, 1, c) for c in late]
    if z > 0:
        out["down"] += [(z + s, 0, c) for s in range(length - z) for c in every]
        if z == length - 1:
            out["down"] += [(z, 1, c) for c in every]
        if z == 1:
            out["down"] += [(z, 1, c) for c in late]
    for b in sorted(range(length), key=lambda b: (abs(b - z), b)):
        pieces = every
        if (z, b) in ((0, 1), (length - 1, length - 2)):
            pieces = early
        if (z, b) in ((1, 0), (length - 2, length - 1)):
            pieces = []
        out["side"] += [(b, 0, c) for c in pieces]
    return out


def order_of(length):
    size = [1.0] * PIECES + [0.1]
    queues = [queues_of(z, length) for z in range(length)]
    far = 1e9
    there = [{} for _ in range(length)]
    for z in range(length):
        for c in range(PIECES + 1):
            there[z][z, 0, c] = 0.0
    for _ in range(4 * length):
        for z in range(length):
            for name, queue in queues[z].items():
                now = 0.0
                for b, o, c in queue:
                    now = max(now, there[z].get((b, o, c), far)) + size[c]
                    to = {"up": z + 1, "down": z - 1, "side": z}[name]
                    key = (b, 1 - o if name == "side" else o, c)
                    there[to][key] = now
    result = []
    for z in range(length):
        events = []
        for name, queue in queues[z].items():
            key = 0.0
            for at, (b, o, c) in enumerate(queue):
                key = max(key, there[z][b, o, c])
                events.append((key, at, name, b, o, c))
        assert max(e[0] for e in events) < far
        result.append((sorted(events), there[z]))
    return result


def gather_kernel(
    n_zero, n_model,
    w_q, w_k, w_v, l_q, l_k, l_v, h_q, h_k, h_v, n_a, n_b,
    s_q, s_k, s_v, factors, norms, g_q, g_k, g_v,
    w_vm, h_vm, stage, lows, sums, scales, na_vm, nb_vm, ns_vm,
    send_sem, recv_sem, load_sem, store_sem, stage_sem, ssend_sem, srecv_sem, nsend_sem, nrecv_sem,
):
    w, low, high, gathered = (w_q, w_k, w_v), (l_q, l_k, l_v), (h_q, h_k, h_v), (g_q, g_k, g_v)
    served = (s_q, s_k, s_v)
    length = n_zero // COLUMNS
    zero, model = lax.axis_index("zero"), lax.axis_index("model")
    place, column = zero // COLUMNS, zero % COLUMNS
    rows, rank = w_q.shape[0], l_q.shape[0]
    half = rows // 2
    count = n_zero * n_model
    me = zero * n_model + model

    loads = []
    for m in range(3):
        into = lows.at[zero, pl.ds(m * rank, rank)]
        loads.append(pltpu.make_async_copy(low[m], into, load_sem.at[m]))
    for m in range(3):
        loads.append(pltpu.make_async_copy(w[m], w_vm.at[m], load_sem.at[3 + m]))
        loads.append(pltpu.make_async_copy(high[m], h_vm.at[m], load_sem.at[6 + m]))
    loads.append(pltpu.make_async_copy(n_a, na_vm, load_sem.at[9]))
    loads.append(pltpu.make_async_copy(n_b, nb_vm, load_sem.at[10]))
    for load in loads:
        load.start()

    barrier = pltpu.get_barrier_semaphore()

    def greet(k, carry):
        to = lax.rem(me + k, count)
        pl.semaphore_signal(
            barrier, inc=1, device_id=(to // n_model, to % n_model), device_id_type=MESH
        )
        return carry

    lax.fori_loop(1, count, greet, 0)
    pl.semaphore_wait(barrier, count - 1)
    for load in loads:
        load.wait()

    def block_at(b, o):
        return b * COLUMNS + (column if o == 0 else 1 - column)

    def landing(block, c):
        if c < PIECES:
            first = pl.multiple_of(block * rows, rows) + (c % 2) * half
            return gathered[c // 2].at[pl.ds(pl.multiple_of(first, half), half)]
        return lows.at[block]

    lane_of = {"up": 0, "down": 1, "side": 2}

    def copy_of(z, name, at, b, o, c):
        block = block_at(b, o)
        target = {
            "up": (z + 1) * COLUMNS + column,
            "down": (z - 1) * COLUMNS + column,
            "side": z * COLUMNS + 1 - column,
        }[name]
        source = landing(block, c)
        if b == z and o == 0 and c < PIECES:
            source = w[c // 2].at[pl.ds((c % 2) * half, half)]
        return pltpu.make_async_remote_copy(
            src_ref=source,
            dst_ref=landing(block, c),
            send_sem=send_sem.at[lane_of[name], at],
            recv_sem=recv_sem.at[block, c],
            device_id=(target, model),
            device_id_type=MESH,
        )

    def arrive(b, o, c):
        block = block_at(b, o)
        pltpu.make_async_copy(
            landing(block, c), landing(block, c), recv_sem.at[block, c]
        ).wait()

    def send_own(pieces):
        for z in range(length):

            @pl.when(place == z)
            def _(z=z):
                for key, at, name, b, o, c in orders[z][0]:
                    if b == z and o == 0 and c in pieces:
                        copy_of(z, name, at, b, o, c).start()

    orders = order_of(length)
    send_own((PIECES, *range(FIRST)))

    def whole_of(m, block, source, at):
        mixed = lax.dot_general(
            lows[block, pl.ds(m * rank, rank), at],
            h_vm[m],
            (((0,), (0,)), ((), ())),
            preferred_element_type=jnp.float32,
        )
        return source[at, :].astype(jnp.float32) + mix_rate * mixed

    tile = 128
    ns_vm[...] = na_vm[...] + nb_vm[...]
    for m in range(3):

        def add(i, total, m=m):
            at = pl.ds(pl.multiple_of(i * tile, tile), tile)
            whole = whole_of(m, zero, w_vm.at[m], at)
            return total + jnp.sum(
                jnp.abs(whole).reshape(tile // 8, 8, whole.shape[1]), axis=0
            )

        total = lax.fori_loop(
            0, rows // tile, add, jnp.zeros((8, w_vm.shape[2]), jnp.float32)
        )
        sums[zero, m : m + 1, :] = jnp.sum(total, axis=0, keepdims=True)

    def sum_copy(k):
        to = lax.rem(zero + k, n_zero)
        return pltpu.make_async_remote_copy(
            src_ref=sums.at[zero],
            dst_ref=sums.at[zero],
            send_sem=ssend_sem.at[k],
            recv_sem=srecv_sem.at[zero],
            device_id=(to, model),
            device_id_type=MESH,
        )

    def norm_copy(k):
        to = lax.rem(me + k, count)
        return pltpu.make_async_remote_copy(
            src_ref=ns_vm,
            dst_ref=norms.at[me],
            send_sem=nsend_sem.at[k],
            recv_sem=nrecv_sem.at[me],
            device_id=(to // n_model, to % n_model),
            device_id_type=MESH,
        )

    for k in range(1, n_zero):
        sum_copy(k).start()
    send_own(tuple(range(FIRST, PIECES)))

    def send_norm(k, carry):
        norm_copy(k).start()
        return carry

    lax.fori_loop(1, count, send_norm, 0)
    own_norm = pltpu.make_async_copy(ns_vm, norms.at[me], store_sem)
    own_norm.start()

    for k in range(1, n_zero):
        origin = lax.rem(zero + k, n_zero)
        pltpu.make_async_copy(sums.at[origin], sums.at[origin], srecv_sem.at[origin]).wait()
        sum_copy(k).wait_send()
    factor = jnp.sum(sums[...], axis=0) / (rows * n_zero)
    factors[...] = factor
    scales[...] = 1.0 / factor

    def finish(m, block, source):
        base = pl.multiple_of(block * rows, rows)

        def step(i, carry):
            first = pl.multiple_of(i * tile, tile)
            whole = whole_of(m, block, source, pl.ds(first, tile))
            to = pl.ds(pl.multiple_of(base + first, tile), tile)
            served[m][to, :] = (whole * scales[m : m + 1, :]).astype(s_q.dtype)
            return carry

        lax.fori_loop(0, rows // tile, step, 0)

    for m in range(3):
        finish(m, zero, w_vm.at[m])

    for z in range(length):

        @pl.when(place == z)
        def _(z=z):
            events, there = orders[z]
            items = [(key, 0, at, name, b, o, c) for key, at, name, b, o, c in events]
            for b in range(length):
                for o in range(COLUMNS):
                    if (b, o) != (z, 0):
                        for m in range(3):
                            when = max(there[b, o, c] for c in (2 * m, 2 * m + 1, PIECES))
                            items.append((when, 1, m, "", b, o, 0))
            seen = set()

            def need(b, o, c):
                if (b, o) != (z, 0) and (b, o, c) not in seen:
                    seen.add((b, o, c))
                    arrive(b, o, c)

            for _, kind, at, name, b, o, c in sorted(items):
                if kind == 0:
                    if (b, o) != (z, 0):
                        need(b, o, c)
                        copy_of(z, name, at, b, o, c).start()
                    continue
                for piece in (2 * at, 2 * at + 1, PIECES):
                    need(b, o, piece)
                block = block_at(b, o)
                raw = gathered[at].at[pl.ds(pl.multiple_of(block * rows, rows), rows)]
                load = pltpu.make_async_copy(raw, stage, stage_sem)
                load.start()
                load.wait()
                finish(at, block, stage)
            for key, at, name, b, o, c in events:
                copy_of(z, name, at, b, o, c).wait_send()

    own_norm.wait()

    def end_norm(k, carry):
        norm_copy(k).wait_send()
        origin = lax.rem(me + k, count)
        pltpu.make_async_copy(norms.at[origin], norms.at[origin], nrecv_sem.at[origin]).wait()
        return carry

    lax.fori_loop(1, count, end_norm, 0)


def write_kernel(s_q, s_k, s_v, factors, o_q, o_k, o_v, f_q, f_k, f_v, sem):
    rows = s_q.shape[0] // WRITES
    copies = []
    for m, (s, o) in enumerate(((s_q, o_q), (s_k, o_k), (s_v, o_v))):
        for i in range(WRITES):
            part = pl.ds(i * rows, rows)
            copies.append(pltpu.make_async_copy(s.at[part], o.at[part], sem.at[m * WRITES + i]))
            copies[-1].start()
    for m, f in enumerate((f_q, f_k, f_v)):
        f[...] = factors[m : m + 1, :]
    for copy in copies:
        copy.wait()


def on_lines(n_zero, n_model, w_q, l_q, h_q, w_k, l_k, h_k, w_v, l_v, h_v, n_a, n_b):
    rows, width = w_q.shape
    rank = l_q.shape[1]
    d_model = rows * n_zero
    count = n_zero * n_model
    share = n_a.shape[0]
    sends = (n_zero // COLUMNS) * (PIECES + 1) + PIECES
    f32, bf16 = jnp.float32, jnp.bfloat16
    shape = jax.ShapeDtypeStruct
    anywhere = pl.BlockSpec(memory_space=pl.ANY)
    inside = pl.BlockSpec(memory_space=pltpu.VMEM)
    dma = pltpu.SemaphoreType.DMA
    tall = (d_model, width)
    s_q, s_k, s_v, factors, norms, _, _, _ = pl.pallas_call(
        functools.partial(gather_kernel, n_zero, n_model),
        out_shape=(pltpu.VMEM(tall, bf16),) * 3
        + (shape((3, width), f32), shape((count, 1, share), f32))
        + (shape(tall, bf16),) * 3,
        in_specs=[anywhere] * 11,
        out_specs=(inside,) * 4 + (anywhere,) * 4,
        scratch_shapes=[
            pltpu.VMEM((3, rows, width), bf16),
            pltpu.VMEM((3, rank, width), bf16),
            pltpu.VMEM((rows, width), bf16),
            pltpu.VMEM((n_zero, 3 * rank, rows), bf16),
            pltpu.VMEM((n_zero, 3, width), f32),
            pltpu.VMEM((3, width), f32),
            pltpu.VMEM((1, share), f32),
            pltpu.VMEM((1, share), f32),
            pltpu.VMEM((1, share), f32),
            dma((3, sends)),
            dma((n_zero, PIECES + 1)),
            dma((11,)),
            dma,
            dma,
            dma((n_zero,)),
            dma((n_zero,)),
            dma((count,)),
            dma((count,)),
        ],
        compiler_params=pltpu.CompilerParams(
            collective_id=0, has_side_effects=True, vmem_limit_bytes=VMEM_MOST - 3 * d_model * width * 2 - SPARE
        ),
    )(w_q, w_k, w_v, l_q.T, l_k.T, l_v.T, h_q, h_k, h_v, n_a.reshape(1, share), n_b.reshape(1, share))
    *served, f_q, f_k, f_v = pl.pallas_call(
        write_kernel,
        out_shape=(shape(tall, bf16),) * 3 + (shape((1, width), f32),) * 3,
        in_specs=[anywhere] * 3 + [inside],
        out_specs=(anywhere,) * 3 + (inside,) * 3,
        scratch_shapes=[dma((3 * WRITES,))],
        compiler_params=pltpu.CompilerParams(
            vmem_limit_bytes=4 * 1024 * 1024
        ),
    )(s_q, s_k, s_v, factors)
    norm = norms.astype(bf16).reshape(count * share)
    return (*served, f_q.reshape(width), f_k.reshape(width), f_v.reshape(width), norm)


def plain(n_zero, n_model, w_q, l_q, h_q, w_k, l_k, h_k, w_v, l_v, h_v, n_a, n_b):
    d_model = w_q.shape[0] * n_zero
    wholes = [
        w.astype(jnp.float32) + mix_rate * jnp.dot(l, h, preferred_element_type=jnp.float32)
        for w, l, h in ((w_q, l_q, h_q), (w_k, l_k, h_k), (w_v, l_v, h_v))
    ]
    totals = lax.psum([jnp.sum(jnp.abs(whole), axis=0) for whole in wholes], "zero")
    factors = [total / d_model for total in totals]
    serving = [
        lax.all_gather((whole / factor).astype(jnp.bfloat16), "zero", axis=0, tiled=True)
        for whole, factor in zip(wholes, factors)
    ]
    norm = lax.all_gather(
        (n_a + n_b).astype(jnp.bfloat16), ("zero", "model"), axis=0, tiled=True
    )
    return (*serving, *factors, norm)


def solution(mesh):
    n_zero, n_model = mesh.shape["zero"], mesh.shape["model"]
    lines = n_zero == 2 * n_model
    tall, low, wide = P("zero", "model"), P("zero", None), P(None, "model")
    return jax.shard_map(
        functools.partial(on_lines if lines else plain, n_zero, n_model),
        mesh=mesh,
        in_specs=(tall, low, wide) * 3 + (P(("zero", "model")),) * 2,
        out_specs=(wide,) * 3 + (P("model"),) * 3 + (P(),),
        check_vma=False,
    )
```

profile of v0, /device:TPU:0, one launch (start us, length us, event | category | flops | bytes accessed | tf_op | source)
XLA Modules:
  0.0 269.6 jit_solution(8408627951677945322)
XLA Ops:
  0.6 258.5 %shard_map.162 = (bf16[4096,1024]{1,0:T(8,128)(2,1)S(1)}, bf16[4096,1024]{1,0:T(8,128)(2,1)S(1)}, bf16[4096,1024]{1,0:T(8,128)(2,1)S(1)}, f32[3,1024]{1,0:T(4,12...) custom-call(bf16[512,1024]{1,0:T(8,128)(2,1)} %w_q.1, ...), custom_call_target="tpu_custom_call" | custom-call | tf_op jit(solution)/shard_map/pallas_call | solution.py:324
  259.1 0.0 copy-start
  259.1 0.7 copy-done
  259.8 0.0 copy-start.1
  259.8 9.1 %shard_map.163 = (bf16[4096,1024]{1,0:T(8,128)(2,1)}, bf16[4096,1024]{1,0:T(8,128)(2,1)}, bf16[4096,1024]{1,0:T(8,128)(2,1)}, f32[1,1024]{1,0:T(1,128)}, f32[1,1024]{1,0:T(1,128)}, /*index=5*/f32[1,1024]{1,0:T(1,128)}) custom-call(bf16[4096,1024]{1,0:T(8,128)(2,1)S(1)} %get-tuple-element.18.s_q, bf16[4096,1024]{1,0:T(8,128)(2,1)S(1)} %get-tuple-element.19.s_k, ...), custom_call_target="tpu_custom_call" | custom-call | tf_op jit(solution)/shard_map/pallas_call | solution.py:355
  268.9 0.0 copy-done.1
  268.9 0.6 convert_reduce_fusion
Async XLA Ops:
  259.1 0.7 copy-start
  259.8 9.1 %copy-start.1 = (f32[32,1,128]{2,1,0:T(1,128)S(1)}, f32[32,1,128]{2,1,0:T(1,128)}, u32[]{:S(2)}) copy-start(f32[32,1,128]{2,1,0:T(1,128)} %get-tuple-element.28) | copy-start | bytes 49156
where the time goes:
time: 271 us; the launch traced here: 270 us
  Pallas kernels  268 us (99%)
    pallas_call x1, Pallas kernels, on_lines(): pl.pallas_call(functools.partial(gather_kernel, n_zero, n_model), out_sha...  258 us
    pallas_call x1, Pallas kernels, on_lines(): pl.pallas_call(write_kernel, out_shape=(shape(tall, bf16),) * 3 + (shape(...  9.08 us

commit v1 on v0

v1 whole, which is shorter than its diff:
```python
import functools

import jax
import jax.numpy as jnp
from jax import lax
from jax.experimental import pallas as pl
from jax.experimental.pallas import tpu as pltpu
from jax.sharding import PartitionSpec as P

MESH = pl.DeviceIdType.MESH
mix_rate = 0.5
VMEM_MOST = 67_043_328
SPARE = 65_536
COLUMNS = 2
PIECES = 6
RAW = 2
LOW, NORM = PIECES, PIECES + 1
WRITES = 4
FIRST = 1


def queues_of(z, length):
    every = [LOW] + list(range(PIECES)) + [NORM]
    late = list(range(PIECES // 2, PIECES))
    early = [c for c in every if c not in late]
    out = {"up": [], "down": [], "side": []}
    if z < length - 1:
        out["up"] += [(z - s, 0, c) for s in range(z + 1) for c in every]
        if z == 0:
            out["up"] += [(0, 1, c) for c in every]
        if z == length - 2:
            out["up"] += [(z, 1, c) for c in late]
    if z > 0:
        out["down"] += [(z + s, 0, c) for s in range(length - z) for c in every]
        if z == length - 1:
            out["down"] += [(z, 1, c) for c in every]
        if z == 1:
            out["down"] += [(z, 1, c) for c in late]
    for b in sorted(range(length), key=lambda b: (abs(b - z), b)):
        pieces = every
        if (z, b) in ((0, 1), (length - 1, length - 2)):
            pieces = early
        if (z, b) in ((1, 0), (length - 2, length - 1)):
            pieces = []
        out["side"] += [(b, 0, c) for c in pieces]
    return out


def order_of(length):
    size = [1.0] * PIECES + [0.04, 0.01]
    queues = [queues_of(z, length) for z in range(length)]
    far = 1e9
    there = [{} for _ in range(length)]
    for z in range(length):
        for c in range(len(size)):
            there[z][z, 0, c] = 0.0
    for _ in range(4 * length):
        for z in range(length):
            for name, queue in queues[z].items():
                now = 0.0
                for b, o, c in queue:
                    now = max(now, there[z].get((b, o, c), far)) + size[c]
                    to = {"up": z + 1, "down": z - 1, "side": z}[name]
                    key = (b, 1 - o if name == "side" else o, c)
                    there[to][key] = now
    result = []
    for z in range(length):
        events = []
        for name, queue in queues[z].items():
            key = 0.0
            for at, (b, o, c) in enumerate(queue):
                key = max(key, there[z][b, o, c])
                events.append((key, at, name, b, o, c))
        assert max(e[0] for e in events) < far
        result.append((sorted(events), there[z]))
    return result


def gather_kernel(
    n_zero, n_model,
    w_q, w_k, w_v, l_q, l_k, l_v, h_q, h_k, h_v, n_a, n_b,
    s_q, s_k, s_v, factors, norms,
    w_vm, h_vm, l_vm, lows, raws, sums, scales, na_vm, nb_vm,
    send_sem, recv_sem, load_sem, ssend_sem, srecv_sem, nsend_sem, nrecv_sem, ready_sem,
):
    w, low, high = (w_q, w_k, w_v), (l_q, l_k, l_v), (h_q, h_k, h_v)
    served = (s_q, s_k, s_v)
    length = n_zero // COLUMNS
    zero, model = lax.axis_index("zero"), lax.axis_index("model")
    place, column = zero // COLUMNS, zero % COLUMNS
    rows, width = w_q.shape
    rank = l_q.shape[0]
    half = rows // 2
    me = zero * n_model + model
    orders = order_of(length)

    barrier = pltpu.get_barrier_semaphore()
    partners = [(zero, lax.rem(model + k, n_model)) for k in range(1, n_model)]
    partners.append((place * COLUMNS + 1 - column, model))
    for to in partners:
        pl.semaphore_signal(barrier, inc=1, device_id=to, device_id_type=MESH)

    @pl.when(place > 0)
    def _():
        pl.semaphore_signal(barrier, inc=1, device_id=(zero - COLUMNS, model), device_id_type=MESH)

    @pl.when(place < length - 1)
    def _():
        pl.semaphore_signal(barrier, inc=1, device_id=(zero + COLUMNS, model), device_id_type=MESH)

    loads = []
    for m in range(3):
        into = lows.at[zero] if m == 0 else l_vm.at[m - 1]
        loads.append(pltpu.make_async_copy(low[m], into, load_sem.at[m]))
    for m in range(3):
        loads.append(pltpu.make_async_copy(w[m], w_vm.at[m], load_sem.at[3 + m]))
        loads.append(pltpu.make_async_copy(high[m], h_vm.at[m], load_sem.at[6 + m]))
    loads.append(pltpu.make_async_copy(n_a, na_vm, load_sem.at[9]))
    loads.append(pltpu.make_async_copy(n_b, nb_vm, load_sem.at[10]))
    for load in loads:
        load.start()

    def block_at(b, o):
        return b * COLUMNS + (column if o == 0 else 1 - column)

    def part(ref, block, c):
        first = pl.multiple_of(block * rows, rows) + (c % 2) * half
        return ref.at[pl.ds(pl.multiple_of(first, half), half)]

    def landing(block, c):
        if c == LOW:
            return lows.at[block]
        if c == NORM:
            return norms.at[pl.ds(block * n_model, n_model)]
        return part(raws if c < RAW else served[c // 2], block, c)

    lane_of = {"up": 0, "down": 1, "side": 2}

    def copy_of(z, name, at, b, o, c):
        block = block_at(b, o)
        target = {
            "up": (z + 1) * COLUMNS + column,
            "down": (z - 1) * COLUMNS + column,
            "side": z * COLUMNS + 1 - column,
        }[name]
        source = landing(block, c)
        if b == z and o == 0:
            if c < RAW:
                source = w_q.at[pl.ds((c % 2) * half, half)]
            if c == LOW:
                source = l_q
        return pltpu.make_async_remote_copy(
            src_ref=source,
            dst_ref=landing(block, c),
            send_sem=send_sem.at[lane_of[name], at],
            recv_sem=recv_sem.at[block, c],
            device_id=(target, model),
            device_id_type=MESH,
        )

    def arrive(b, o, c):
        block = block_at(b, o)
        pltpu.make_async_copy(
            landing(block, c), landing(block, c), recv_sem.at[block, c]
        ).wait()

    def send_own(z, pieces):
        for key, at, name, b, o, c in orders[z][0]:
            if b == z and o == 0 and c in pieces:
                copy_of(z, name, at, b, o, c).start()

    def ready(z, way):
        pl.semaphore_signal(
            ready_sem.at[way], inc=1, device_id=(zero + (1 - 2 * way) * COLUMNS, model), device_id_type=MESH
        )

    for z in range(length):

        @pl.when(place == z)
        def _(z=z):
            pl.semaphore_wait(barrier, len(partners) + (z > 0) + (z < length - 1))
            send_own(z, (LOW, *range(FIRST)))
            if z > 0:
                pl.semaphore_wait(ready_sem.at[0], 1)
            if z < length - 1:
                ready(z, 0)
                pl.semaphore_wait(ready_sem.at[1], 1)
            if z > 0:
                ready(z, 1)

    for load in loads:
        load.wait()

    def whole_of(m, low_ref, source, at):
        mixed = lax.dot_general(
            low_ref[:, at], h_vm[m], (((0,), (0,)), ((), ())), preferred_element_type=jnp.float32
        )
        return source[at, :].astype(jnp.float32) + mix_rate * mixed

    def own_low(m):
        return lows.at[zero] if m == 0 else l_vm.at[m - 1]

    tile = 128
    for m in range(3):

        def add(i, total, m=m):
            at = pl.ds(pl.multiple_of(i * tile, tile), tile)
            whole = whole_of(m, own_low(m), w_vm.at[m], at)
            return total + jnp.sum(jnp.abs(whole).reshape(tile // 8, 8, width), axis=0)

        total = lax.fori_loop(0, rows // tile, add, jnp.zeros((8, width), jnp.float32))
        sums[zero, :, m * width : (m + 1) * width] = jnp.sum(total, axis=0, keepdims=True)
    norms[pl.ds(me, 1)] = (na_vm[...] + nb_vm[...])[None]

    def sum_copy(k):
        to = lax.rem(zero + k, n_zero)
        return pltpu.make_async_remote_copy(
            src_ref=sums.at[zero],
            dst_ref=sums.at[zero],
            send_sem=ssend_sem.at[k],
            recv_sem=srecv_sem.at[zero],
            device_id=(to, model),
            device_id_type=MESH,
        )

    def norm_copy(k):
        return pltpu.make_async_remote_copy(
            src_ref=norms.at[me],
            dst_ref=norms.at[me],
            send_sem=nsend_sem.at[k],
            recv_sem=nrecv_sem.at[model],
            device_id=partners[k - 1],
            device_id_type=MESH,
        )

    for k in range(1, n_zero):
        sum_copy(k).start()
    for z in range(length):

        @pl.when(place == z)
        def _(z=z):
            send_own(z, tuple(range(FIRST, RAW)))

    for k in range(1, n_model):
        norm_copy(k).start()

    for k in range(1, n_zero):
        origin = lax.rem(zero + k, n_zero)
        pltpu.make_async_copy(sums.at[origin], sums.at[origin], srecv_sem.at[origin]).wait()
    total = sums[0]
    for b in range(1, n_zero):
        total = total + sums[b]
    factor = total / (rows * n_zero)
    factors[...] = factor
    scales[...] = 1.0 / factor

    def finish(m, block, low_ref, source):
        base = pl.multiple_of(block * rows, rows)

        def step(i, carry):
            first = pl.multiple_of(i * tile, tile)
            whole = whole_of(m, low_ref, source, pl.ds(first, tile))
            to = pl.ds(pl.multiple_of(base + first, tile), tile)
            served[m][to, :] = (whole * scales[:, m * width : (m + 1) * width]).astype(s_q.dtype)
            return carry

        lax.fori_loop(0, rows // tile, step, 0)

    for m in (1, 2, 0):
        finish(m, zero, own_low(m), w_vm.at[m])
    for k in range(1, n_model):
        origin = lax.rem(model + k, n_model)
        mine = norms.at[zero * n_model + origin]
        pltpu.make_async_copy(mine, mine, nrecv_sem.at[origin]).wait()

    for z in range(length):

        @pl.when(place == z)
        def _(z=z):
            send_own(z, (*range(RAW, PIECES), NORM))
            events, there = orders[z]
            items = [(key, 0, at, name, b, o, c) for key, at, name, b, o, c in events]
            for b in range(length):
                for o in range(COLUMNS):
                    if (b, o) != (z, 0):
                        when = max(there[b, o, c] for c in (*range(RAW), LOW))
                        items.append((when, 1, 0, "", b, o, 0))
            seen = set()

            def need(b, o, c):
                if (b, o) != (z, 0) and (b, o, c) not in seen:
                    seen.add((b, o, c))
                    arrive(b, o, c)

            for _, kind, at, name, b, o, c in sorted(items):
                if kind == 0:
                    if (b, o) != (z, 0):
                        need(b, o, c)
                        copy_of(z, name, at, b, o, c).start()
                    continue
                for piece in (*range(RAW), LOW):
                    need(b, o, piece)
                block = block_at(b, o)
                raw = raws.at[pl.ds(pl.multiple_of(block * rows, rows), rows)]
                finish(0, block, lows.at[block], raw)
            for b in range(length):
                for o in range(COLUMNS):
                    for c in range(PIECES + 2):
                        need(b, o, c)
            for key, at, name, b, o, c in events:
                copy_of(z, name, at, b, o, c).wait_send()

    for k in range(1, n_zero):
        sum_copy(k).wait_send()
    for k in range(1, n_model):
        norm_copy(k).wait_send()


def write_kernel(s_q, s_k, s_v, factors, norms, o_q, o_k, o_v, f_q, f_k, f_v, norm, sem):
    rows = s_q.shape[0] // WRITES
    width = s_q.shape[1]
    copies = []
    for m, (s, o) in enumerate(((s_q, o_q), (s_k, o_k), (s_v, o_v))):
        for i in range(WRITES):
            part = pl.ds(i * rows, rows)
            copies.append(pltpu.make_async_copy(s.at[part], o.at[part], sem.at[m * WRITES + i]))
            copies[-1].start()
    for m, f in enumerate((f_q, f_k, f_v)):
        f[...] = factors[:, m * width : (m + 1) * width]
    norm[...] = norms[...].reshape(norm.shape).astype(norm.dtype)
    for copy in copies:
        copy.wait()


def on_lines(n_zero, n_model, w_q, l_q, h_q, w_k, l_k, h_k, w_v, l_v, h_v, n_a, n_b):
    rows, width = w_q.shape
    rank = l_q.shape[1]
    d_model = rows * n_zero
    count = n_zero * n_model
    share = n_a.shape[0]
    sends = (n_zero // COLUMNS) * (PIECES + 2) + PIECES
    f32, bf16 = jnp.float32, jnp.bfloat16
    shape = jax.ShapeDtypeStruct
    anywhere = pl.BlockSpec(memory_space=pl.ANY)
    inside = pl.BlockSpec(memory_space=pltpu.VMEM)
    dma = pltpu.SemaphoreType.DMA
    tall = (d_model, width)
    s_q, s_k, s_v, factors, norms = pl.pallas_call(
        functools.partial(gather_kernel, n_zero, n_model),
        out_shape=(pltpu.VMEM(tall, bf16),) * 3
        + (pltpu.VMEM((1, 3 * width), f32), pltpu.VMEM((count, 1, share), f32)),
        in_specs=[anywhere] * 11,
        out_specs=(inside,) * 5,
        scratch_shapes=[
            pltpu.VMEM((3, rows, width), bf16),
            pltpu.VMEM((3, rank, width), bf16),
            pltpu.VMEM((2, rank, rows), bf16),
            pltpu.VMEM((n_zero, rank, rows), bf16),
            pltpu.VMEM(tall, bf16),
            pltpu.VMEM((n_zero, 1, 3 * width), f32),
            pltpu.VMEM((1, 3 * width), f32),
            pltpu.VMEM((1, share), f32),
            pltpu.VMEM((1, share), f32),
            dma((3, sends)),
            dma((n_zero, PIECES + 2)),
            dma((11,)),
            dma((n_zero,)),
            dma((n_zero,)),
            dma((n_model,)),
            dma((n_model,)),
            pltpu.SemaphoreType.REGULAR((2,)),
        ],
        compiler_params=pltpu.CompilerParams(
            collective_id=0, has_side_effects=True, vmem_limit_bytes=VMEM_MOST - 3 * d_model * width * 2 - SPARE
        ),
    )(w_q, w_k, w_v, l_q.T, l_k.T, l_v.T, h_q, h_k, h_v, n_a.reshape(1, share), n_b.reshape(1, share))
    *served, f_q, f_k, f_v, norm = pl.pallas_call(
        write_kernel,
        out_shape=(shape(tall, bf16),) * 3 + (shape((1, width), f32),) * 3 + (shape((count, share), bf16),),
        in_specs=[anywhere] * 3 + [inside] * 2,
        out_specs=(anywhere,) * 3 + (inside,) * 4,
        scratch_shapes=[dma((3 * WRITES,))],
        compiler_params=pltpu.CompilerParams(
            vmem_limit_bytes=4 * 1024 * 1024
        ),
    )(s_q, s_k, s_v, factors, norms)
    return (*served, f_q.reshape(width), f_k.reshape(width), f_v.reshape(width), norm.reshape(count * share))


def plain(n_zero, n_model, w_q, l_q, h_q, w_k, l_k, h_k, w_v, l_v, h_v, n_a, n_b):
    d_model = w_q.shape[0] * n_zero
    wholes = [
        w.astype(jnp.float32) + mix_rate * jnp.dot(l, h, preferred_element_type=jnp.float32)
        for w, l, h in ((w_q, l_q, h_q), (w_k, l_k, h_k), (w_v, l_v, h_v))
    ]
    totals = lax.psum([jnp.sum(jnp.abs(whole), axis=0) for whole in wholes], "zero")
    factors = [total / d_model for total in totals]
    serving = [
        lax.all_gather((whole / factor).astype(jnp.bfloat16), "zero", axis=0, tiled=True)
        for whole, factor in zip(wholes, factors)
    ]
    norm = lax.all_gather(
        (n_a + n_b).astype(jnp.bfloat16), ("zero", "model"), axis=0, tiled=True
    )
    return (*serving, *factors, norm)


def solution(mesh):
    n_zero, n_model = mesh.shape["zero"], mesh.shape["model"]
    lines = n_zero == 2 * n_model
    tall, low, wide = P("zero", "model"), P("zero", None), P(None, "model")
    return jax.shard_map(
        functools.partial(on_lines if lines else plain, n_zero, n_model),
        mesh=mesh,
        in_specs=(tall, low, wide) * 3 + (P(("zero", "model")),) * 2,
        out_specs=(wide,) * 3 + (P("model"),) * 3 + (P(),),
        check_vma=False,
    )
```

time: 271 us -> 256 us (0.945)
  Pallas kernels: 268 us -> 256 us
    pallas_call x1, Pallas kernels: 258 us -> 247 us  [on_lines(): pl.pallas_call(functools.partial(gather_kernel, n_zero, n_model), out_sha...]
where the time goes in v1:
time: 256 us
  Pallas kernels  256 us (100%)
    pallas_call x1, Pallas kernels, on_lines(): pl.pallas_call(functools.partial(gather_kernel, n_zero, n_model), out_sha...  247 us
    pallas_call x1, Pallas kernels, on_lines(): pl.pallas_call(write_kernel, out_shape=(shape(tall, bf16),) * 3 + (shape(...  9.09 us

profile of v1, /device:TPU:0, one launch (start us, length us, event | category | flops | bytes accessed | tf_op | source)
XLA Modules:
  0.0 256.3 jit_solution(14121539434618912870)
XLA Ops:
  0.6 246.5 %shard_map.162 = (bf16[4096,1024]{1,0:T(8,128)(2,1)S(1)}, bf16[4096,1024]{1,0:T(8,128)(2,1)S(1)}, bf16[4096,1024]{1,0:T(8,128)(2,1)S(1)}, f32[1,3072]{1,0:T(1,128)S(1)}, f32[32,1,128]{2,1,0:T(1,128)S(1)}) custom-call(bf16[512,1024]{1,0:T(8,128)(2,1)} %w_q.1, bf16[512,1024]{1,0:T(8,128)(2,1)} %w_k.1, bf16[512,1024]{1,0:T(8,128)(2,1)} %w_v.1, ...), custom_call_target="tpu_custom_call" | custom-call | tf_op jit(solution)/shard_map/pallas_call | solution.py:348
  247.2 9.1 %shard_map.163 = (bf16[4096,1024]{1,0:T(8,128)(2,1)}, bf16[4096,1024]{1,0:T(8,128)(2,1)}, bf16[4096,1024]{1,0:T(8,128)(2,1)}, f32[1,1024]{1,0:T(1,128)}, f32[1,1...) custom-call(bf16[4096,1024]{1,0:T(8,128)(2,1)S(1)} %get-tuple-element.19.s_q, ...), custom_call_target="tpu_custom_call" | custom-call | tf_op jit(solution)/shard_map/pallas_call | solution.py:377

commit v2 on v1

--- a/solution.py
+++ b/solution.py
@@ -12,8 +12,10 @@
 VMEM_MOST = 67_043_328
 SPARE = 65_536
 COLUMNS = 2
-PIECES = 6
+PARTS = ((0, 0, 1), (0, 1, 1), (0, 2, 2), (1, 0, 2), (1, 2, 2), (2, 0, 2), (2, 2, 2))
+PIECES = len(PARTS)
 RAW = 2
+LATE = (4, 5, 6)
 LOW, NORM = PIECES, PIECES + 1
 WRITES = 4
 FIRST = 1
@@ -21,7 +23,7 @@
 
 def queues_of(z, length):
     every = [LOW] + list(range(PIECES)) + [NORM]
-    late = list(range(PIECES // 2, PIECES))
+    late = list(LATE)
     early = [c for c in every if c not in late]
     out = {"up": [], "down": [], "side": []}
     if z < length - 1:
@@ -47,7 +49,7 @@
 
 
 def order_of(length):
-    size = [1.0] * PIECES + [0.04, 0.01]
+    size = [part[2] / 2 for part in PARTS] + [0.02, 0.01]
     queues = [queues_of(z, length) for z in range(length)]
     far = 1e9
     there = [{} for _ in range(length)]
@@ -80,8 +82,8 @@
     n_zero, n_model,
     w_q, w_k, w_v, l_q, l_k, l_v, h_q, h_k, h_v, n_a, n_b,
     s_q, s_k, s_v, factors, norms,
-    w_vm, h_vm, l_vm, lows, raws, sums, scales, na_vm, nb_vm,
-    send_sem, recv_sem, load_sem, ssend_sem, srecv_sem, nsend_sem, nrecv_sem, ready_sem,
+    w_vm, h_vm, l_vm, lows, raws, sums, scales, n_vm,
+    send_sem, recv_sem, load_sem, sum_sem, norm_sem, ready_sem,
 ):
     w, low, high = (w_q, w_k, w_v), (l_q, l_k, l_v), (h_q, h_k, h_v)
     served = (s_q, s_k, s_v)
@@ -90,7 +92,8 @@
     place, column = zero // COLUMNS, zero % COLUMNS
     rows, width = w_q.shape
     rank = l_q.shape[0]
-    half = rows // 2
+    quarter = rows // 4
+    raw_rows = raws.shape[0] // n_zero
     me = zero * n_model + model
     orders = order_of(length)
 
@@ -108,35 +111,35 @@
     def _():
         pl.semaphore_signal(barrier, inc=1, device_id=(zero + COLUMNS, model), device_id_type=MESH)
 
-    loads = []
-    for m in range(3):
-        into = lows.at[zero] if m == 0 else l_vm.at[m - 1]
-        loads.append(pltpu.make_async_copy(low[m], into, load_sem.at[m]))
-    for m in range(3):
-        loads.append(pltpu.make_async_copy(w[m], w_vm.at[m], load_sem.at[3 + m]))
-        loads.append(pltpu.make_async_copy(high[m], h_vm.at[m], load_sem.at[6 + m]))
-    loads.append(pltpu.make_async_copy(n_a, na_vm, load_sem.at[9]))
-    loads.append(pltpu.make_async_copy(n_b, nb_vm, load_sem.at[10]))
-    for load in loads:
-        load.start()
+    for i, (refs, into) in enumerate(((low, l_vm), (w, w_vm), (high, h_vm), ((n_a, n_b), n_vm))):
+        for m, ref in enumerate(refs):
+            pltpu.make_async_copy(ref, into.at[m], load_sem.at[i]).start()
 
     def block_at(b, o):
         return b * COLUMNS + (column if o == 0 else 1 - column)
-
-    def part(ref, block, c):
-        first = pl.multiple_of(block * rows, rows) + (c % 2) * half
-        return ref.at[pl.ds(pl.multiple_of(first, half), half)]
 
     def landing(block, c):
         if c == LOW:
             return lows.at[block]
         if c == NORM:
             return norms.at[pl.ds(block * n_model, n_model)]
-        return part(raws if c < RAW else served[c // 2], block, c)
-
-    lane_of = {"up": 0, "down": 1, "side": 2}
-
-    def copy_of(z, name, at, b, o, c):
+        m, first, many = PARTS[c]
+        ref, tall = (raws, raw_rows) if c < RAW else (served[m], rows)
+        first = pl.multiple_of(block * tall, quarter) + first * quarter
+        return ref.at[pl.ds(pl.multiple_of(first, quarter), many * quarter)]
+
+    def taken(ref, sem):
+        pltpu.make_async_copy(ref, ref, sem).wait()
+
+    def group_of(name, c):
+        if c in (LOW, NORM):
+            return 6 + c - LOW
+        return PARTS[c][0] + 3 * (name == "side")
+
+    def arrival(block, at, c):
+        return recv_sem.at[lax.rem(block - at + n_zero - 1, n_zero), c]
+
+    def copy_of(z, name, b, o, c):
         block = block_at(b, o)
         target = {
             "up": (z + 1) * COLUMNS + column,
@@ -146,28 +149,34 @@
         source = landing(block, c)
         if b == z and o == 0:
             if c < RAW:
-                source = w_q.at[pl.ds((c % 2) * half, half)]
+                m, first, many = PARTS[c]
+                source = w[m].at[pl.ds(first * quarter, many * quarter)]
             if c == LOW:
-                source = l_q
+                source = l_q.at[:, pl.ds(0, raw_rows)]
         return pltpu.make_async_remote_copy(
             src_ref=source,
             dst_ref=landing(block, c),
-            send_sem=send_sem.at[lane_of[name], at],
-            recv_sem=recv_sem.at[block, c],
+            send_sem=send_sem.at[group_of(name, c)],
+            recv_sem=arrival(block, target, c),
             device_id=(target, model),
             device_id_type=MESH,
         )
 
     def arrive(b, o, c):
         block = block_at(b, o)
-        pltpu.make_async_copy(
-            landing(block, c), landing(block, c), recv_sem.at[block, c]
-        ).wait()
+        taken(landing(block, c), arrival(block, zero, c))
 
     def send_own(z, pieces):
         for key, at, name, b, o, c in orders[z][0]:
             if b == z and o == 0 and c in pieces:
-                copy_of(z, name, at, b, o, c).start()
+                copy_of(z, name, b, o, c).start()
+
+    def send_all(pieces):
+        for z in range(length):
+
+            @pl.when(place == z)
+            def _(z=z):
+                send_own(z, pieces)
 
     def ready(z, way):
         pl.semaphore_signal(
@@ -180,16 +189,23 @@
         def _(z=z):
             pl.semaphore_wait(barrier, len(partners) + (z > 0) + (z < length - 1))
             send_own(z, (LOW, *range(FIRST)))
-            if z > 0:
-                pl.semaphore_wait(ready_sem.at[0], 1)
-            if z < length - 1:
-                ready(z, 0)
-                pl.semaphore_wait(ready_sem.at[1], 1)
-            if z > 0:
-                ready(z, 1)
-
-    for load in loads:
-        load.wait()
+            for way in (0, 1):
+                if (length - 1 - z, z)[way] and not (z, length - 1 - z)[way]:
+                    ready(z, way)
+
+    def relay(step):
+        for z in range(length):
+            way = step if z < length // 2 else 1 - step
+
+            @pl.when(place == z)
+            def _(z=z, way=way):
+                if (z, length - 1 - z)[way]:
+                    pl.semaphore_wait(ready_sem.at[way], 1)
+                    if (length - 1 - z, z)[way]:
+                        ready(z, way)
+
+    for i, into in enumerate((l_vm, w_vm, h_vm, n_vm)):
+        taken(into, load_sem.at[i])
 
     def whole_of(m, low_ref, source, at):
         mixed = lax.dot_general(
@@ -197,28 +213,27 @@
         )
         return source[at, :].astype(jnp.float32) + mix_rate * mixed
 
-    def own_low(m):
-        return lows.at[zero] if m == 0 else l_vm.at[m - 1]
-
     tile = 128
     for m in range(3):
 
         def add(i, total, m=m):
             at = pl.ds(pl.multiple_of(i * tile, tile), tile)
-            whole = whole_of(m, own_low(m), w_vm.at[m], at)
+            whole = whole_of(m, l_vm.at[m], w_vm.at[m], at)
             return total + jnp.sum(jnp.abs(whole).reshape(tile // 8, 8, width), axis=0)
 
         total = lax.fori_loop(0, rows // tile, add, jnp.zeros((8, width), jnp.float32))
         sums[zero, :, m * width : (m + 1) * width] = jnp.sum(total, axis=0, keepdims=True)
-    norms[pl.ds(me, 1)] = (na_vm[...] + nb_vm[...])[None]
+        if m < 2:
+            relay(m)
+    norms[pl.ds(me, 1)] = (n_vm[0] + n_vm[1])[None]
 
     def sum_copy(k):
         to = lax.rem(zero + k, n_zero)
         return pltpu.make_async_remote_copy(
             src_ref=sums.at[zero],
             dst_ref=sums.at[zero],
-            send_sem=ssend_sem.at[k],
-            recv_sem=srecv_sem.at[zero],
+            send_sem=sum_sem.at[0],
+            recv_sem=sum_sem.at[1],
             device_id=(to, model),
             device_id_type=MESH,
         )
@@ -227,26 +242,19 @@
         return pltpu.make_async_remote_copy(
             src_ref=norms.at[me],
             dst_ref=norms.at[me],
-            send_sem=nsend_sem.at[k],
-            recv_sem=nrecv_sem.at[model],
+            send_sem=norm_sem.at[0],
+            recv_sem=norm_sem.at[1],
             device_id=partners[k - 1],
             device_id_type=MESH,
         )
 
     for k in range(1, n_zero):
         sum_copy(k).start()
-    for z in range(length):
-
-        @pl.when(place == z)
-        def _(z=z):
-            send_own(z, tuple(range(FIRST, RAW)))
-
+    send_all(tuple(range(FIRST, RAW)))
     for k in range(1, n_model):
         norm_copy(k).start()
 
-    for k in range(1, n_zero):
-        origin = lax.rem(zero + k, n_zero)
-        pltpu.make_async_copy(sums.at[origin], sums.at[origin], srecv_sem.at[origin]).wait()
+    taken(sums.at[pl.ds(0, n_zero - 1)], sum_sem.at[1])
     total = sums[0]
     for b in range(1, n_zero):
         total = total + sums[b]
@@ -254,30 +262,35 @@
     factors[...] = factor
     scales[...] = 1.0 / factor
 
-    def finish(m, block, low_ref, source):
+    def finish(m, block, low_ref, source, start, many):
         base = pl.multiple_of(block * rows, rows)
 
         def step(i, carry):
-            first = pl.multiple_of(i * tile, tile)
+            first = pl.multiple_of(start + i * tile, tile)
             whole = whole_of(m, low_ref, source, pl.ds(first, tile))
             to = pl.ds(pl.multiple_of(base + first, tile), tile)
             served[m][to, :] = (whole * scales[:, m * width : (m + 1) * width]).astype(s_q.dtype)
             return carry
 
-        lax.fori_loop(0, rows // tile, step, 0)
-
-    for m in (1, 2, 0):
-        finish(m, zero, own_low(m), w_vm.at[m])
-    for k in range(1, n_model):
-        origin = lax.rem(model + k, n_model)
-        mine = norms.at[zero * n_model + origin]
-        pltpu.make_async_copy(mine, mine, nrecv_sem.at[origin]).wait()
+        lax.fori_loop(0, many // tile, step, 0)
+
+    def finish_own(m, start, many):
+        finish(m, zero, l_vm.at[m], w_vm.at[m], start, many)
+
+    finish_own(0, raw_rows, rows - raw_rows)
+    finish_own(1, 0, rows)
+    send_all(tuple(c for c in range(RAW, PIECES) if PARTS[c][0] == 0))
+    finish_own(2, 0, rows)
+    send_all(tuple(c for c in range(RAW, PIECES) if PARTS[c][0] == 1))
+    finish_own(0, 0, raw_rows)
+    send_all(tuple(c for c in range(RAW, PIECES) if PARTS[c][0] == 2))
+    taken(norms.at[pl.ds(0, n_model - 1)], norm_sem.at[1])
 
     for z in range(length):
 
         @pl.when(place == z)
         def _(z=z):
-            send_own(z, (*range(RAW, PIECES), NORM))
+            send_own(z, (NORM,))
             events, there = orders[z]
             items = [(key, 0, at, name, b, o, c) for key, at, name, b, o, c in events]
             for b in range(length):
@@ -296,38 +309,45 @@
                 if kind == 0:
                     if (b, o) != (z, 0):
                         need(b, o, c)
-                        copy_of(z, name, at, b, o, c).start()
+                        copy_of(z, name, b, o, c).start()
                     continue
                 for piece in (*range(RAW), LOW):
                     need(b, o, piece)
                 block = block_at(b, o)
-                raw = raws.at[pl.ds(pl.multiple_of(block * rows, rows), rows)]
-                finish(0, block, lows.at[block], raw)
+                raw = raws.at[pl.ds(pl.multiple_of(block * raw_rows, raw_rows), raw_rows)]
+                finish(0, block, lows.at[block], raw, 0, raw_rows)
             for b in range(length):
                 for o in range(COLUMNS):
                     for c in range(PIECES + 2):
                         need(b, o, c)
+            sent = [0] * 8
             for key, at, name, b, o, c in events:
-                copy_of(z, name, at, b, o, c).wait_send()
-
-    for k in range(1, n_zero):
-        sum_copy(k).wait_send()
-    for k in range(1, n_model):
-        norm_copy(k).wait_send()
-
-
-def write_kernel(s_q, s_k, s_v, factors, norms, o_q, o_k, o_v, f_q, f_k, f_v, norm, sem):
+                sent[group_of(name, c)] += 1 if c in (LOW, NORM) else PARTS[c][2] * quarter
+            sent[7] *= n_model
+            for i, many in enumerate(sent):
+                if many:
+                    taken((lows, norms)[i - 6].at[pl.ds(0, many)] if i > 5 else s_q.at[pl.ds(0, many)], send_sem.at[i])
+
+    taken(sums.at[pl.ds(0, n_zero - 1)], sum_sem.at[0])
+    taken(norms.at[pl.ds(0, n_model - 1)], norm_sem.at[0])
+
+
+def write_kernel(s_q, s_k, s_v, factors, norms, o_q, o_k, o_v, f_q, f_k, f_v, norm, norm_vm, sem):
     rows = s_q.shape[0] // WRITES
     width = s_q.shape[1]
     copies = []
     for m, (s, o) in enumerate(((s_q, o_q), (s_k, o_k), (s_v, o_v))):
         for i in range(WRITES):
             part = pl.ds(i * rows, rows)
-            copies.append(pltpu.make_async_copy(s.at[part], o.at[part], sem.at[m * WRITES + i]))
-            copies[-1].start()
+            copies.append((s.at[part], o.at[part]))
     for m, f in enumerate((f_q, f_k, f_v)):
-        f[...] = factors[:, m * width : (m + 1) * width]
-    norm[...] = norms[...].reshape(norm.shape).astype(norm.dtype)
+        copies.append((factors.at[:, pl.ds(m * width, width)], f))
+    copies.append((norm_vm, norm))
+    copies = [pltpu.make_async_copy(s, o, sem.at[i]) for i, (s, o) in enumerate(copies)]
+    for copy in copies[:-1]:
+        copy.start()
+    norm_vm[...] = norms[...].reshape(norm.shape).astype(norm.dtype)
+    copies[-1].start()
     for copy in copies:
         copy.wait()
 
@@ -338,7 +358,7 @@
     d_model = rows * n_zero
     count = n_zero * n_model
     share = n_a.shape[0]
-    sends = (n_zero // COLUMNS) * (PIECES + 2) + PIECES
+    raw_rows = sum(part[2] for part in PARTS[:RAW]) * rows // 4
     f32, bf16 = jnp.float32, jnp.bfloat16
     shape = jax.ShapeDtypeStruct
     anywhere = pl.BlockSpec(memory_space=pl.ANY)
@@ -354,20 +374,17 @@
         scratch_shapes=[
             pltpu.VMEM((3, rows, width), bf16),
             pltpu.VMEM((3, rank, width), bf16),
-            pltpu.VMEM((2, rank, rows), bf16),
-            pltpu.VMEM((n_zero, rank, rows), bf16),
-            pltpu.VMEM(tall, bf16),
+            pltpu.VMEM((3, rank, rows), bf16),
+            pltpu.VMEM((n_zero, rank, raw_rows), bf16),
+            pltpu.VMEM((n_zero * raw_rows, width), bf16),
             pltpu.VMEM((n_zero, 1, 3 * width), f32),
             pltpu.VMEM((1, 3 * width), f32),
-            pltpu.VMEM((1, share), f32),
-            pltpu.VMEM((1, share), f32),
-            dma((3, sends)),
-            dma((n_zero, PIECES + 2)),
-            dma((11,)),
-            dma((n_zero,)),
-            dma((n_zero,)),
-            dma((n_model,)),
-            dma((n_model,)),
+            pltpu.VMEM((2, 1, share), f32),
+            dma((8,)),
+            dma((n_zero - 1, PIECES + 2)),
+            dma((4,)),
+            dma((2,)),
+            dma((2,)),
             pltpu.SemaphoreType.REGULAR((2,)),
         ],
         compiler_params=pltpu.CompilerParams(
@@ -378,8 +395,8 @@
         write_kernel,
         out_shape=(shape(tall, bf16),) * 3 + (shape((1, width), f32),) * 3 + (shape((count, share), bf16),),
         in_specs=[anywhere] * 3 + [inside] * 2,
-        out_specs=(anywhere,) * 3 + (inside,) * 4,
-        scratch_shapes=[dma((3 * WRITES,))],
+        out_specs=(anywhere,) * 7,
+        scratch_shapes=[pltpu.VMEM((count, share), bf16), dma((3 * WRITES + 4,))],
         compiler_params=pltpu.CompilerParams(
             vmem_limit_bytes=4 * 1024 * 1024
         ),

time: 256 us -> 254 us (level)
  Pallas kernels: 256 us -> 253 us
where the time goes in v2:
time: 254 us
  Pallas kernels  253 us (100%)
    pallas_call x1, Pallas kernels, on_lines(): pl.pallas_call(functools.partial(gather_kernel, n_zero, n_model), out_sha...  245 us
    pallas_call x1, Pallas kernels, on_lines(): pl.pallas_call(write_kernel, out_shape=(shape(tall, bf16),) * 3 + (shape(...  8.53 us

profile of v2, /device:TPU:0, one launch (start us, length us, event | category | flops | bytes accessed | tf_op | source)
XLA Modules:
  0.0 253.9 jit_solution(3546690386642677240)
XLA Ops:
  0.6 244.8 %shard_map.162 = (bf16[4096,1024]{1,0:T(8,128)(2,1)S(1)}, bf16[4096,1024]{1,0:T(8,128)(2,1)S(1)}, bf16[4096,1024]{1,0:T(8,128)(2,1)S(1)}, f32[1,3072]{1,0:T(1,128)S(1)}, f32[32,1,128]{2,1,0:T(1,128)S(1)}) custom-call(bf16[512,1024]{1,0:T(8,128)(2,1)} %w_q.1, bf16[512,1024]{1,0:T(8,128)(2,1)} %w_k.1, bf16[512,1024]{1,0:T(8,128)(2,1)} %w_v.1, ...), custom_call_target="tpu_custom_call" | custom-call | tf_op jit(solution)/shard_map/pallas_call | solution.py:368
  245.4 8.5 %shard_map.163 = (bf16[4096,1024]{1,0:T(8,128)(2,1)}, bf16[4096,1024]{1,0:T(8,128)(2,1)}, bf16[4096,1024]{1,0:T(8,128)(2,1)}, f32[1,1024]{1,0:T(1,128)}, f32[1,1...) custom-call(bf16[4096,1024]{1,0:T(8,128)(2,1)S(1)} %get-tuple-element.19.s_q, ...), custom_call_target="tpu_custom_call" | custom-call | tf_op jit(solution)/shard_map/pallas_call | solution.py:394

commit v3 on v2

--- a/solution.py
+++ b/solution.py
@@ -12,16 +12,25 @@
 VMEM_MOST = 67_043_328
 SPARE = 65_536
 COLUMNS = 2
-PARTS = ((0, 0, 1), (0, 1, 1), (0, 2, 2), (1, 0, 2), (1, 2, 2), (2, 0, 2), (2, 2, 2))
+PARTS = ((0, 0, 1), (0, 1, 1), (0, 2, 2), (1, 0, 2), (1, 2, 2), (2, 0, 1), (2, 1, 3))
 PIECES = len(PARTS)
 RAW = 2
 LATE = (4, 5, 6)
+LAST = 6
+CORES = 2
 LOW, NORM = PIECES, PIECES + 1
 WRITES = 4
 FIRST = 1
 
 
-def queues_of(z, length):
+def last_of(z, core, length):
+    end, inner = (0, 1) if z < length // 2 else (length - 1, length - 2)
+    if core == 0:
+        return (inner, 1) if z == end else None, (inner, 1) if z == inner else None
+    return (length - 1 - end, 1) if z == end else None, (length - 1 - end, 0) if z == end else None
+
+
+def queues_of(z, core, length):
     every = [LOW] + list(range(PIECES)) + [NORM]
     late = list(LATE)
     early = [c for c in every if c not in late]
@@ -45,12 +54,16 @@
         if (z, b) in ((1, 0), (length - 2, length - 1)):
             pieces = []
         out["side"] += [(b, 0, c) for c in pieces]
+    _, handed = last_of(z, core, length)
+    if handed:
+        name = "side" if core else "down" if z < length // 2 else "up"
+        out[name].remove((*handed, LAST))
     return out
 
 
-def order_of(length):
+def order_of(core, length):
     size = [part[2] / 2 for part in PARTS] + [0.02, 0.01]
-    queues = [queues_of(z, length) for z in range(length)]
+    queues = [queues_of(z, core, length) for z in range(length)]
     far = 1e9
     there = [{} for _ in range(length)]
     for z in range(length):
@@ -81,7 +94,7 @@
 def gather_kernel(
     n_zero, n_model,
     w_q, w_k, w_v, l_q, l_k, l_v, h_q, h_k, h_v, n_a, n_b,
-    s_q, s_k, s_v, factors, norms,
+    s_q, s_k, s_v, factors, norms, hand,
     w_vm, h_vm, l_vm, lows, raws, sums, scales, n_vm,
     send_sem, recv_sem, load_sem, sum_sem, norm_sem, ready_sem,
 ):
@@ -95,7 +108,8 @@
     quarter = rows // 4
     raw_rows = raws.shape[0] // n_zero
     me = zero * n_model + model
-    orders = order_of(length)
+    orders = [order_of(core, length) for core in range(CORES)]
+    core_at = model % CORES
 
     barrier = pltpu.get_barrier_semaphore()
     partners = [(zero, lax.rem(model + k, n_model)) for k in range(1, n_model)]
@@ -167,7 +181,7 @@
         taken(landing(block, c), arrival(block, zero, c))
 
     def send_own(z, pieces):
-        for key, at, name, b, o, c in orders[z][0]:
+        for key, at, name, b, o, c in orders[0][z][0]:
             if b == z and o == 0 and c in pieces:
                 copy_of(z, name, b, o, c).start()
 
@@ -286,47 +300,69 @@
     send_all(tuple(c for c in range(RAW, PIECES) if PARTS[c][0] == 2))
     taken(norms.at[pl.ds(0, n_model - 1)], norm_sem.at[1])
 
-    for z in range(length):
-
-        @pl.when(place == z)
-        def _(z=z):
-            send_own(z, (NORM,))
-            events, there = orders[z]
-            items = [(key, 0, at, name, b, o, c) for key, at, name, b, o, c in events]
-            for b in range(length):
-                for o in range(COLUMNS):
-                    if (b, o) != (z, 0):
-                        when = max(there[b, o, c] for c in (*range(RAW), LOW))
-                        items.append((when, 1, 0, "", b, o, 0))
-            seen = set()
-
-            def need(b, o, c):
-                if (b, o) != (z, 0) and (b, o, c) not in seen:
-                    seen.add((b, o, c))
-                    arrive(b, o, c)
-
-            for _, kind, at, name, b, o, c in sorted(items):
-                if kind == 0:
-                    if (b, o) != (z, 0):
-                        need(b, o, c)
-                        copy_of(z, name, b, o, c).start()
-                    continue
+    send_all((NORM,))
+
+    def hand_on(b, o):
+        block = block_at(b, o)
+        m, first, many = PARTS[LAST]
+        base = pl.multiple_of(block * rows, rows) + first * quarter
+
+        def step(i, carry):
+            at = pl.multiple_of(i * tile, tile)
+            hand[pl.ds(at, tile), :] = served[m][pl.ds(pl.multiple_of(base + at, tile), tile), :]
+            return carry
+
+        lax.fori_loop(0, many * quarter // tile, step, 0)
+
+    def serve(z, core):
+        events, there = orders[core][z]
+        lacking, handed = last_of(z, core, length)
+        items = [(key, 0, name, b, o, c) for key, at, name, b, o, c in events]
+        for b in range(length):
+            for o in range(COLUMNS):
+                if (b, o) != (z, 0):
+                    when = max(there[b, o, c] for c in (*range(RAW), LOW))
+                    items.append((when, 1, "", b, o, 0))
+        if handed:
+            items.append((there[(*handed, LAST)], 2, "", *handed, LAST))
+        seen = {(z, 0, c) for c in range(PIECES + 2)}
+        if lacking:
+            seen.add((*lacking, LAST))
+
+        def need(b, o, c):
+            if (b, o, c) not in seen:
+                seen.add((b, o, c))
+                arrive(b, o, c)
+
+        for _, kind, name, b, o, c in sorted(items):
+            if kind == 0:
+                if (b, o) != (z, 0):
+                    need(b, o, c)
+                    copy_of(z, name, b, o, c).start()
+            elif kind == 1:
                 for piece in (*range(RAW), LOW):
                     need(b, o, piece)
                 block = block_at(b, o)
                 raw = raws.at[pl.ds(pl.multiple_of(block * raw_rows, raw_rows), raw_rows)]
                 finish(0, block, lows.at[block], raw, 0, raw_rows)
-            for b in range(length):
-                for o in range(COLUMNS):
-                    for c in range(PIECES + 2):
-                        need(b, o, c)
-            sent = [0] * 8
-            for key, at, name, b, o, c in events:
-                sent[group_of(name, c)] += 1 if c in (LOW, NORM) else PARTS[c][2] * quarter
-            sent[7] *= n_model
-            for i, many in enumerate(sent):
-                if many:
-                    taken((lows, norms)[i - 6].at[pl.ds(0, many)] if i > 5 else s_q.at[pl.ds(0, many)], send_sem.at[i])
+            else:
+                need(b, o, c)
+                hand_on(b, o)
+        for b in range(length):
+            for o in range(COLUMNS):
+                for c in range(PIECES + 2):
+                    need(b, o, c)
+        sent = [0] * 8
+        for key, at, name, b, o, c in events:
+            sent[group_of(name, c)] += 1 if c in (LOW, NORM) else PARTS[c][2] * quarter
+        sent[7] *= n_model
+        for i, many in enumerate(sent):
+            if many:
+                taken((lows, norms)[i - 6].at[pl.ds(0, many)] if i > 5 else s_q.at[pl.ds(0, many)], send_sem.at[i])
+
+    for z in range(length):
+        for core in range(CORES):
+            pl.when((place == z) & (core_at == core))(functools.partial(serve, z, core))
 
     taken(sums.at[pl.ds(0, n_zero - 1)], sum_sem.at[0])
     taken(norms.at[pl.ds(0, n_model - 1)], norm_sem.at[0])
@@ -352,6 +388,26 @@
         copy.wait()
 
 
+def last_kernel(n_zero, n_model, given, late, out, sem):
+    length = n_zero // COLUMNS
+    zero, model = lax.axis_index("zero"), lax.axis_index("model")
+    place, column, core_at = zero // COLUMNS, zero % COLUMNS, model % CORES
+    rows = out.shape[0] // n_zero
+    first = PARTS[LAST][1] * (rows // 4)
+    for z in (0, length - 1):
+        for core in range(CORES):
+            lacking, _ = last_of(z, core, length)
+
+            @pl.when((place == z) & (core_at == core))
+            def _(b=lacking[0]):
+                block = b * COLUMNS + 1 - column
+                base = pl.multiple_of(block * rows, rows) + first
+                part = out.at[pl.ds(pl.multiple_of(base, rows // 4), late.shape[0])]
+                copy = pltpu.make_async_copy(late, part, sem)
+                copy.start()
+                copy.wait()
+
+
 def on_lines(n_zero, n_model, w_q, l_q, h_q, w_k, l_k, h_k, w_v, l_v, h_v, n_a, n_b):
     rows, width = w_q.shape
     rank = l_q.shape[1]
@@ -365,12 +421,13 @@
     inside = pl.BlockSpec(memory_space=pltpu.VMEM)
     dma = pltpu.SemaphoreType.DMA
     tall = (d_model, width)
-    s_q, s_k, s_v, factors, norms = pl.pallas_call(
+    hand_rows = PARTS[LAST][2] * rows // 4
+    s_q, s_k, s_v, factors, norms, hand = pl.pallas_call(
         functools.partial(gather_kernel, n_zero, n_model),
         out_shape=(pltpu.VMEM(tall, bf16),) * 3
-        + (pltpu.VMEM((1, 3 * width), f32), pltpu.VMEM((count, 1, share), f32)),
+        + (pltpu.VMEM((1, 3 * width), f32), pltpu.VMEM((count, 1, share), f32), pltpu.VMEM((hand_rows, width), bf16)),
         in_specs=[anywhere] * 11,
-        out_specs=(inside,) * 5,
+        out_specs=(inside,) * 6,
         scratch_shapes=[
             pltpu.VMEM((3, rows, width), bf16),
             pltpu.VMEM((3, rank, width), bf16),
@@ -388,9 +445,18 @@
             pltpu.SemaphoreType.REGULAR((2,)),
         ],
         compiler_params=pltpu.CompilerParams(
-            collective_id=0, has_side_effects=True, vmem_limit_bytes=VMEM_MOST - 3 * d_model * width * 2 - SPARE
+            collective_id=0, has_side_effects=True, vmem_limit_bytes=VMEM_MOST - 3 * d_model * width * 2 - 8 * hand_rows * width - SPARE
         ),
     )(w_q, w_k, w_v, l_q.T, l_k.T, l_v.T, h_q, h_k, h_v, n_a.reshape(1, share), n_b.reshape(1, share))
+    pairs = []
+    for zero in range(n_zero):
+        for model in range(n_model):
+            z, column, core = zero // COLUMNS, zero % COLUMNS, model % CORES
+            lacking, _ = last_of(z, core, n_zero // COLUMNS)
+            if lacking:
+                giver = (z * COLUMNS + 1 - column) if core else lacking[0] * COLUMNS + column
+                pairs.append((giver * n_model + model, zero * n_model + model))
+    late = lax.ppermute(hand, ("zero", "model"), pairs)
     *served, f_q, f_k, f_v, norm = pl.pallas_call(
         write_kernel,
         out_shape=(shape(tall, bf16),) * 3 + (shape((1, width), f32),) * 3 + (shape((count, share), bf16),),
@@ -400,7 +466,17 @@
         compiler_params=pltpu.CompilerParams(
             vmem_limit_bytes=4 * 1024 * 1024
         ),
+        cost_estimate=pl.CostEstimate(flops=10**9, bytes_accessed=12 * d_model * width, transcendentals=0),
     )(s_q, s_k, s_v, factors, norms)
+    served[2] = pl.pallas_call(
+        functools.partial(last_kernel, n_zero, n_model),
+        out_shape=shape(tall, bf16),
+        in_specs=[anywhere] * 2,
+        out_specs=anywhere,
+        scratch_shapes=[dma],
+        input_output_aliases={0: 0},
+        compiler_params=pltpu.CompilerParams(vmem_limit_bytes=1024 * 1024),
+    )(served[2], late)
     return (*served, f_q.reshape(width), f_k.reshape(width), f_v.reshape(width), norm.reshape(count * share))
 
 

time: 254 us -> 252 us (level)
  Pallas kernels: 253 us -> 245 us
  waiting for transfers between devices: 0 us -> 4.05 us
    pallas_call x1, Pallas kernels: 245 us -> 236 us  [on_lines(): pl.pallas_call(functools.partial(gather_kernel, n_zero, n_model), out_sha...]
    ppermute x0 -> x1, waiting for transfers between devices: none -> 4.05 us  [on_lines(): late = lax.ppermute(hand, ('zero', 'model'), pairs)]
  transfers between devices with their start and end apart: 0 -> 1, of which waited for: 0 -> 1; matrix products, arithmetic and copies ran while one was open for 0% -> 0% of each run, Pallas kernels for 0% -> 3%
where the time goes in v3:
time: 252 us; the launch traced here: 251 us
  Pallas kernels  245 us (97%)
  waiting for transfers between devices  4.05 us (2%)
    pallas_call x1, Pallas kernels, on_lines(): pl.pallas_call(functools.partial(gather_kernel, n_zero, n_model), out_sha...  236 us
    pallas_call x1, Pallas kernels, on_lines(): pl.pallas_call(write_kernel, out_shape=(shape(tall, bf16),) * 3 + (shape(...  8.53 us
  transfers between devices with their start and end apart: 1, of which 1 were waited for; matrix products, arithmetic and copies ran while one was open for 0% of the time, Pallas kernels for 3%

profile of v3, /device:TPU:0, one launch (start us, length us, event | category | flops | bytes accessed | tf_op | source)
XLA Modules:
  0.0 251.3 jit_solution(13464266755510313858)
XLA Ops:
  0.6 235.9 %shard_map.162 = (bf16[4096,1024]{1,0:T(8,128)(2,1)S(1)}, bf16[4096,1024]{1,0:T(8,128)(2,1)S(1)}, bf16[4096,1024]{1,0:T(8,128)(2,1)S(1)}, f32[1,3072]{1,0:T(1,12...) custom-call(bf16[512,1024]{1,0:T(8,128)(2,1)} %w_q.1, bf16[512,1024]{1,0:T(8,128)(2,1)} %w_k.1, ...), custom_call_target="tpu_custom_call" | custom-call | tf_op jit(solution)/shard_map/pallas_call | solution.py:425
  236.5 1.3 collective-permute-start
  237.8 8.5 %shard_map.163 = (bf16[4096,1024]{1,0:T(8,128)(2,1)}, bf16[4096,1024]{1,0:T(8,128)(2,1)}, bf16[4096,1024]{1,0:T(8,128)(2,1)}, f32[1,1024]{1,0:T(1,128)}, f32[1,1...) custom-call(bf16[4096,1024]{1,0:T(8,128)(2,1)S(1)} %get-tuple-element.20.s_q, ...), custom_call_target="tpu_custom_call" | custom-call | flops 1000000000 | bytes 50331648 | tf_op jit(solution)/shard_map/pallas_call | solution.py:460
  246.4 4.0 %collective-permute-done.late = bf16[384,1024]{1,0:T(8,128)(2,1)S(1)} collective-permute-done((bf16[384,1024]{1,0:T(8,128)(2,1)S(1)}, bf16[384,1024]{1,0:T(8,128)(2,1)S(1)}, u32[]{:S(2)}, u32[]{:S(2)}) %collective-permute-start) | collective-permute-done | bytes 786464 | tf_op jit(solution)/shard_map/ppermute | solution.py:459
  250.4 0.9 shard_map.164
Async XLA Ops:
  236.5 13.9 %collective-permute-start = (bf16[384,1024]{1,0:T(8,128)(2,1)S(1)}, bf16[384,1024]{1,0:T(8,128)(2,1)S(1)}, u32[]{:S(2)}, u32[]{:S(2)}) collective-permute-start(bf16[384,1024]{1,0:T(8,128)(2,1)S(1)} %get-tuple-element.28), channel_id=1, source_target_pairs={{8,0},{5,1},{10,2},{7,3},{12,4},{1,5},{14,6},{3,7},{16,24},{29,25}... | collective-permute-start | bytes 2359304 | tf_op jit(solution)/shard_map/ppermute | solution.py:459

commit v4 on v3

--- a/solution.py
+++ b/solution.py
@@ -31,7 +31,7 @@
 
 
 def queues_of(z, core, length):
-    every = [LOW] + list(range(PIECES)) + [NORM]
+    every = [LOW, *range(RAW + 1), NORM, *range(RAW + 1, PIECES)]
     late = list(LATE)
     early = [c for c in every if c not in late]
     out = {"up": [], "down": [], "side": []}
@@ -293,15 +293,12 @@
 
     finish_own(0, raw_rows, rows - raw_rows)
     finish_own(1, 0, rows)
-    send_all(tuple(c for c in range(RAW, PIECES) if PARTS[c][0] == 0))
+    taken(norms.at[pl.ds(0, n_model - 1)], norm_sem.at[1])
+    send_all((NORM, *(c for c in range(RAW, PIECES) if PARTS[c][0] == 0)))
     finish_own(2, 0, rows)
     send_all(tuple(c for c in range(RAW, PIECES) if PARTS[c][0] == 1))
     finish_own(0, 0, raw_rows)
     send_all(tuple(c for c in range(RAW, PIECES) if PARTS[c][0] == 2))
-    taken(norms.at[pl.ds(0, n_model - 1)], norm_sem.at[1])
-
-    send_all((NORM,))
-
     def hand_on(b, o):
         block = block_at(b, o)
         m, first, many = PARTS[LAST]
@@ -317,14 +314,14 @@
     def serve(z, core):
         events, there = orders[core][z]
         lacking, handed = last_of(z, core, length)
-        items = [(key, 0, name, b, o, c) for key, at, name, b, o, c in events]
+        items = [(key, 0, at, name, b, o, c) for key, at, name, b, o, c in events]
         for b in range(length):
             for o in range(COLUMNS):
                 if (b, o) != (z, 0):
                     when = max(there[b, o, c] for c in (*range(RAW), LOW))
-                    items.append((when, 1, "", b, o, 0))
+                    items.append((when, 1, 0, "", b, o, 0))
         if handed:
-            items.append((there[(*handed, LAST)], 2, "", *handed, LAST))
+            items.append((there[(*handed, LAST)], 2, 0, "", *handed, LAST))
         seen = {(z, 0, c) for c in range(PIECES + 2)}
         if lacking:
             seen.add((*lacking, LAST))
@@ -334,7 +331,7 @@
                 seen.add((b, o, c))
                 arrive(b, o, c)
 
-        for _, kind, name, b, o, c in sorted(items):
+        for _, kind, _, name, b, o, c in sorted(items):
             if kind == 0:
                 if (b, o) != (z, 0):
                     need(b, o, c)

time: 252 us -> 252 us (level)
  no operation moved by 1% of the time
where the time goes in v4:
time: 252 us; the launch traced here: 251 us
  Pallas kernels  245 us (97%)
  waiting for transfers between devices  4.05 us (2%)
    pallas_call x1, Pallas kernels, on_lines(): pl.pallas_call(functools.partial(gather_kernel, n_zero, n_model), out_sha...  236 us
    pallas_call x1, Pallas kernels, on_lines(): pl.pallas_call(write_kernel, out_shape=(shape(tall, bf16),) * 3 + (shape(...  8.53 us
  transfers between devices with their start and end apart: 1, of which 1 were waited for; matrix products, arithmetic and copies ran while one was open for 0% of the time, Pallas kernels for 3%

profile of v4, /device:TPU:0, one launch (start us, length us, event | category | flops | bytes accessed | tf_op | source)
XLA Modules:
  0.0 251.4 jit_solution(4516371294886040784)
XLA Ops:
  0.6 235.9 %shard_map.162 = (bf16[4096,1024]{1,0:T(8,128)(2,1)S(1)}, bf16[4096,1024]{1,0:T(8,128)(2,1)S(1)}, bf16[4096,1024]{1,0:T(8,128)(2,1)S(1)}, f32[1,3072]{1,0:T(1,12...) custom-call(bf16[512,1024]{1,0:T(8,128)(2,1)} %w_q.1, bf16[512,1024]{1,0:T(8,128)(2,1)} %w_k.1, ...), custom_call_target="tpu_custom_call" | custom-call | tf_op jit(solution)/shard_map/pallas_call | solution.py:422
  236.6 1.3 collective-permute-start
  237.9 8.5 %shard_map.163 = (bf16[4096,1024]{1,0:T(8,128)(2,1)}, bf16[4096,1024]{1,0:T(8,128)(2,1)}, bf16[4096,1024]{1,0:T(8,128)(2,1)}, f32[1,1024]{1,0:T(1,128)}, f32[1,1...) custom-call(bf16[4096,1024]{1,0:T(8,128)(2,1)S(1)} %get-tuple-element.20.s_q, ...), custom_call_target="tpu_custom_call" | custom-call | flops 1000000000 | bytes 50331648 | tf_op jit(solution)/shard_map/pallas_call | solution.py:457
  246.4 4.0 %collective-permute-done.late = bf16[384,1024]{1,0:T(8,128)(2,1)S(1)} collective-permute-done((bf16[384,1024]{1,0:T(8,128)(2,1)S(1)}, bf16[384,1024]{1,0:T(8,128)(2,1)S(1)}, u32[]{:S(2)}, u32[]{:S(2)}) %collective-permute-start) | collective-permute-done | bytes 786464 | tf_op jit(solution)/shard_map/ppermute | solution.py:456
  250.5 0.9 shard_map.164
Async XLA Ops:
  236.6 13.9 %collective-permute-start = (bf16[384,1024]{1,0:T(8,128)(2,1)S(1)}, bf16[384,1024]{1,0:T(8,128)(2,1)S(1)}, u32[]{:S(2)}, u32[]{:S(2)}) collective-permute-start(bf16[384,1024]{1,0:T(8,128)(2,1)S(1)} %get-tuple-element.28), channel_id=1, source_target_pairs={{8,0},{5,1},{10,2},{7,3},{12,4},{1,5},{14,6},{3,7},{16,24},{29,25}... | collective-permute-start | bytes 2359304 | tf_op jit(solution)/shard_map/ppermute | solution.py:456

commit v5 on v4

--- a/solution.py
+++ b/solution.py
@@ -12,7 +12,8 @@
 VMEM_MOST = 67_043_328
 SPARE = 65_536
 COLUMNS = 2
-PARTS = ((0, 0, 1), (0, 1, 1), (0, 2, 2), (1, 0, 2), (1, 2, 2), (2, 0, 1), (2, 1, 3))
+SHARES = 32
+PARTS = ((0, 0, 8), (0, 8, 8), (0, 16, 16), (1, 0, 15), (1, 15, 17), (2, 0, 8), (2, 8, 24))
 PIECES = len(PARTS)
 RAW = 2
 LATE = (4, 5, 6)
@@ -62,7 +63,7 @@
 
 
 def order_of(core, length):
-    size = [part[2] / 2 for part in PARTS] + [0.02, 0.01]
+    size = [part[2] / 16 for part in PARTS] + [0.02, 0.01]
     queues = [queues_of(z, core, length) for z in range(length)]
     far = 1e9
     there = [{} for _ in range(length)]
@@ -105,7 +106,7 @@
     place, column = zero // COLUMNS, zero % COLUMNS
     rows, width = w_q.shape
     rank = l_q.shape[0]
-    quarter = rows // 4
+    share = rows // SHARES
     raw_rows = raws.shape[0] // n_zero
     me = zero * n_model + model
     orders = [order_of(core, length) for core in range(CORES)]
@@ -139,8 +140,8 @@
             return norms.at[pl.ds(block * n_model, n_model)]
         m, first, many = PARTS[c]
         ref, tall = (raws, raw_rows) if c < RAW else (served[m], rows)
-        first = pl.multiple_of(block * tall, quarter) + first * quarter
-        return ref.at[pl.ds(pl.multiple_of(first, quarter), many * quarter)]
+        first = pl.multiple_of(block * tall, share) + first * share
+        return ref.at[pl.ds(pl.multiple_of(first, share), many * share)]
 
     def taken(ref, sem):
         pltpu.make_async_copy(ref, ref, sem).wait()
@@ -164,7 +165,7 @@
         if b == z and o == 0:
             if c < RAW:
                 m, first, many = PARTS[c]
-                source = w[m].at[pl.ds(first * quarter, many * quarter)]
+                source = w[m].at[pl.ds(first * share, many * share)]
             if c == LOW:
                 source = l_q.at[:, pl.ds(0, raw_rows)]
         return pltpu.make_async_remote_copy(
@@ -302,14 +303,14 @@
     def hand_on(b, o):
         block = block_at(b, o)
         m, first, many = PARTS[LAST]
-        base = pl.multiple_of(block * rows, rows) + first * quarter
+        base = pl.multiple_of(block * rows, rows) + first * share
 
         def step(i, carry):
             at = pl.multiple_of(i * tile, tile)
             hand[pl.ds(at, tile), :] = served[m][pl.ds(pl.multiple_of(base + at, tile), tile), :]
             return carry
 
-        lax.fori_loop(0, many * quarter // tile, step, 0)
+        lax.fori_loop(0, many * share // tile, step, 0)
 
     def serve(z, core):
         events, there = orders[core][z]
@@ -351,7 +352,7 @@
                     need(b, o, c)
         sent = [0] * 8
         for key, at, name, b, o, c in events:
-            sent[group_of(name, c)] += 1 if c in (LOW, NORM) else PARTS[c][2] * quarter
+            sent[group_of(name, c)] += 1 if c in (LOW, NORM) else PARTS[c][2] * share
         sent[7] *= n_model
         for i, many in enumerate(sent):
             if many:
@@ -390,7 +391,7 @@
     zero, model = lax.axis_index("zero"), lax.axis_index("model")
     place, column, core_at = zero // COLUMNS, zero % COLUMNS, model % CORES
     rows = out.shape[0] // n_zero
-    first = PARTS[LAST][1] * (rows // 4)
+    first = PARTS[LAST][1] * (rows // SHARES)
     for z in (0, length - 1):
         for core in range(CORES):
             lacking, _ = last_of(z, core, length)
@@ -399,7 +400,7 @@
             def _(b=lacking[0]):
                 block = b * COLUMNS + 1 - column
                 base = pl.multiple_of(block * rows, rows) + first
-                part = out.at[pl.ds(pl.multiple_of(base, rows // 4), late.shape[0])]
+                part = out.at[pl.ds(pl.multiple_of(base, rows // SHARES), late.shape[0])]
                 copy = pltpu.make_async_copy(late, part, sem)
                 copy.start()
                 copy.wait()
@@ -411,14 +412,14 @@
     d_model = rows * n_zero
     count = n_zero * n_model
     share = n_a.shape[0]
-    raw_rows = sum(part[2] for part in PARTS[:RAW]) * rows // 4
+    raw_rows = sum(part[2] for part in PARTS[:RAW]) * rows // SHARES
     f32, bf16 = jnp.float32, jnp.bfloat16
     shape = jax.ShapeDtypeStruct
     anywhere = pl.BlockSpec(memory_space=pl.ANY)
     inside = pl.BlockSpec(memory_space=pltpu.VMEM)
     dma = pltpu.SemaphoreType.DMA
     tall = (d_model, width)
-    hand_rows = PARTS[LAST][2] * rows // 4
+    hand_rows = PARTS[LAST][2] * rows // SHARES
     s_q, s_k, s_v, factors, norms, hand = pl.pallas_call(
         functools.partial(gather_kernel, n_zero, n_model),
         out_shape=(pltpu.VMEM(tall, bf16),) * 3

time: 252 us -> 251 us (level)
  no operation moved by 1% of the time
where the time goes in v5:
time: 251 us
  Pallas kernels  245 us (98%)
  waiting for transfers between devices  4.05 us (2%)
    pallas_call x1, Pallas kernels, on_lines(): pl.pallas_call(functools.partial(gather_kernel, n_zero, n_model), out_sha...  235 us
    pallas_call x1, Pallas kernels, on_lines(): pl.pallas_call(write_kernel, out_shape=(shape(tall, bf16),) * 3 + (shape(...  8.53 us
  transfers between devices with their start and end apart: 1, of which 1 were waited for; matrix products, arithmetic and copies ran while one was open for 0% of the time, Pallas kernels for 3%

profile of v5, /device:TPU:0, one launch (start us, length us, event | category | flops | bytes accessed | tf_op | source)
XLA Modules:
  0.0 250.7 jit_solution(7215260728848783605)
XLA Ops:
  0.6 235.2 %shard_map.162 = (bf16[4096,1024]{1,0:T(8,128)(2,1)S(1)}, bf16[4096,1024]{1,0:T(8,128)(2,1)S(1)}, bf16[4096,1024]{1,0:T(8,128)(2,1)S(1)}, f32[1,3072]{1,0:T(1,12...) custom-call(bf16[512,1024]{1,0:T(8,128)(2,1)} %w_q.1, bf16[512,1024]{1,0:T(8,128)(2,1)} %w_k.1, ...), custom_call_target="tpu_custom_call" | custom-call | tf_op jit(solution)/shard_map/pallas_call | solution.py:423
  235.9 1.3 collective-permute-start
  237.2 8.5 %shard_map.163 = (bf16[4096,1024]{1,0:T(8,128)(2,1)}, bf16[4096,1024]{1,0:T(8,128)(2,1)}, bf16[4096,1024]{1,0:T(8,128)(2,1)}, f32[1,1024]{1,0:T(1,128)}, f32[1,1...) custom-call(bf16[4096,1024]{1,0:T(8,128)(2,1)S(1)} %get-tuple-element.20.s_q, ...), custom_call_target="tpu_custom_call" | custom-call | flops 1000000000 | bytes 50331648 | tf_op jit(solution)/shard_map/pallas_call | solution.py:458
  245.7 4.0 %collective-permute-done.late = bf16[384,1024]{1,0:T(8,128)(2,1)S(1)} collective-permute-done((bf16[384,1024]{1,0:T(8,128)(2,1)S(1)}, bf16[384,1024]{1,0:T(8,128)(2,1)S(1)}, u32[]{:S(2)}, u32[]{:S(2)}) %collective-permute-start) | collective-permute-done | bytes 786464 | tf_op jit(solution)/shard_map/ppermute | solution.py:457
  249.8 0.9 shard_map.164
Async XLA Ops:
  235.9 13.9 %collective-permute-start = (bf16[384,1024]{1,0:T(8,128)(2,1)S(1)}, bf16[384,1024]{1,0:T(8,128)(2,1)S(1)}, u32[]{:S(2)}, u32[]{:S(2)}) collective-permute-start(bf16[384,1024]{1,0:T(8,128)(2,1)S(1)} %get-tuple-element.28), channel_id=1, source_target_pairs={{8,0},{5,1},{10,2},{7,3},{12,4},{1,5},{14,6},{3,7},{16,24},{29,25}... | collective-permute-start | bytes 2359304 | tf_op jit(solution)/shard_map/ppermute | solution.py:457

commit v6 on v5

--- a/solution.py
+++ b/solution.py
@@ -152,7 +152,7 @@
         return PARTS[c][0] + 3 * (name == "side")
 
     def arrival(block, at, c):
-        return recv_sem.at[lax.rem(block - at + n_zero - 1, n_zero), c]
+        return recv_sem.at[lax.rem(block - at + n_zero - 1, n_zero), max(c - RAW + 1, 0)]
 
     def copy_of(z, name, b, o, c):
         block = block_at(b, o)
@@ -179,7 +179,8 @@
 
     def arrive(b, o, c):
         block = block_at(b, o)
-        taken(landing(block, c), arrival(block, zero, c))
+        raw = raws.at[pl.ds(pl.multiple_of(block * raw_rows, raw_rows), raw_rows)]
+        taken(raw if c < RAW else landing(block, c), arrival(block, zero, c))
 
     def send_own(z, pieces):
         for key, at, name, b, o, c in orders[0][z][0]:
@@ -293,9 +294,10 @@
         finish(m, zero, l_vm.at[m], w_vm.at[m], start, many)
 
     finish_own(0, raw_rows, rows - raw_rows)
-    finish_own(1, 0, rows)
+    finish_own(1, 0, rows // 2)
     taken(norms.at[pl.ds(0, n_model - 1)], norm_sem.at[1])
     send_all((NORM, *(c for c in range(RAW, PIECES) if PARTS[c][0] == 0)))
+    finish_own(1, rows // 2, rows // 2)
     finish_own(2, 0, rows)
     send_all(tuple(c for c in range(RAW, PIECES) if PARTS[c][0] == 1))
     finish_own(0, 0, raw_rows)
@@ -329,7 +331,7 @@
 
         def need(b, o, c):
             if (b, o, c) not in seen:
-                seen.add((b, o, c))
+                seen.update((b, o, piece) for piece in (range(RAW) if c < RAW else (c,)))
                 arrive(b, o, c)
 
         for _, kind, _, name, b, o, c in sorted(items):
@@ -436,7 +438,7 @@
             pltpu.VMEM((1, 3 * width), f32),
             pltpu.VMEM((2, 1, share), f32),
             dma((8,)),
-            dma((n_zero - 1, PIECES + 2)),
+            dma((n_zero - 1, PIECES + 3 - RAW)),
             dma((4,)),
             dma((2,)),
             dma((2,)),

time: 251 us -> 251 us (level)
  no operation moved by 1% of the time
where the time goes in v6:
time: 251 us
  Pallas kernels  245 us (98%)
  waiting for transfers between devices  4.05 us (2%)
    pallas_call x1, Pallas kernels, on_lines(): pl.pallas_call(functools.partial(gather_kernel, n_zero, n_model), out_sha...  235 us
    pallas_call x1, Pallas kernels, on_lines(): pl.pallas_call(write_kernel, out_shape=(shape(tall, bf16),) * 3 + (shape(...  8.53 us
  transfers between devices with their start and end apart: 1, of which 1 were waited for; matrix products, arithmetic and copies ran while one was open for 0% of the time, Pallas kernels for 3%

profile of v6, /device:TPU:0, one launch (start us, length us, event | category | flops | bytes accessed | tf_op | source)
XLA Modules:
  0.0 250.6 jit_solution(13471017166496434678)
XLA Ops:
  0.6 235.2 %shard_map.162 = (bf16[4096,1024]{1,0:T(8,128)(2,1)S(1)}, bf16[4096,1024]{1,0:T(8,128)(2,1)S(1)}, bf16[4096,1024]{1,0:T(8,128)(2,1)S(1)}, f32[1,3072]{1,0:T(1,12...) custom-call(bf16[512,1024]{1,0:T(8,128)(2,1)} %w_q.1, bf16[512,1024]{1,0:T(8,128)(2,1)} %w_k.1, ...), custom_call_target="tpu_custom_call" | custom-call | tf_op jit(solution)/shard_map/pallas_call | solution.py:425
  235.8 1.3 collective-permute-start
  237.1 8.5 %shard_map.163 = (bf16[4096,1024]{1,0:T(8,128)(2,1)}, bf16[4096,1024]{1,0:T(8,128)(2,1)}, bf16[4096,1024]{1,0:T(8,128)(2,1)}, f32[1,1024]{1,0:T(1,128)}, f32[1,1...) custom-call(bf16[4096,1024]{1,0:T(8,128)(2,1)S(1)} %get-tuple-element.20.s_q, ...), custom_call_target="tpu_custom_call" | custom-call | flops 1000000000 | bytes 50331648 | tf_op jit(solution)/shard_map/pallas_call | solution.py:460
  245.7 4.0 %collective-permute-done.late = bf16[384,1024]{1,0:T(8,128)(2,1)S(1)} collective-permute-done((bf16[384,1024]{1,0:T(8,128)(2,1)S(1)}, bf16[384,1024]{1,0:T(8,128)(2,1)S(1)}, u32[]{:S(2)}, u32[]{:S(2)}) %collective-permute-start) | collective-permute-done | bytes 786464 | tf_op jit(solution)/shard_map/ppermute | solution.py:459
  249.7 0.9 shard_map.164
Async XLA Ops:
  235.8 13.9 %collective-permute-start = (bf16[384,1024]{1,0:T(8,128)(2,1)S(1)}, bf16[384,1024]{1,0:T(8,128)(2,1)S(1)}, u32[]{:S(2)}, u32[]{:S(2)}) collective-permute-start(bf16[384,1024]{1,0:T(8,128)(2,1)S(1)} %get-tuple-element.28), channel_id=1, source_target_pairs={{8,0},{5,1},{10,2},{7,3},{12,4},{1,5},{14,6},{3,7},{16,24},{29,25}... | collective-permute-start | bytes 2359304 | tf_op jit(solution)/shard_map/ppermute | solution.py:459
